TPU v7x, 128 devices: a whole 4x4x4 slice. The times are simulated.
128 devices in a mesh: chan: 8 (over x, core), tile: 16 (over z, y).
Axes of the slice: x: 4, y: 4, z: 4, core: 2. Of those that a mesh axis runs over, the one named last changes fastest.
Arguments:
- voltages: bfloat16 [8, 2, 2048, 2048], P(None, None, 'tile', 'chan'), may hold values from -16 to 16
- rfi_flags: int32 [8], P('chan'), may hold values 0 or 1
- beam_steer_index: int32 [8, 8], P('chan'), may hold values from 0 to 2047
- start_columns: int32 [8, 32], P('chan'), may hold values from 0 to 2047, as said below
Outputs:
- covariance: float32 [8, 2, 2048, 2048], P('chan', None, 'tile')
- weights: float32 [8, 8, 2, 2048], P('chan', None, None, 'tile')
Inputs may be any that keep to these rules, and one draw needn't show every extreme that they name: `start_columns`: the 32 antenna numbers of one channel are distinct.
All inputs are finite; a program needn't handle non-finite values. No bound on the sum of `rfi_flags` on one device may be relied on, other than what follows from the above.
Results may differ from a plain program's by a relative error of at most 0.0003.
Values may be sent and summed in bfloat16 or wider, within the bound.
No kernel may reach another device: no remote copies, remote signals or barrier semaphores. Data moves between devices by JAX's collectives and lax.ppermute only.
A program may use at most 128 MiB of HBM per device.

v0:
```python
import functools
import math

import jax
import jax.numpy as jnp
from jax import lax
from jax.sharding import Mesh
from jax.sharding import PartitionSpec as P

ARRAY_ELEMENTS = 2048
SNAPSHOT_COUNT = 2048
SUB_ITERS = 4
CG_ITERS = 12
TILE = ("tile_0", "tile_1")


diagonal_loading = 0.1
highest = lax.Precision.HIGHEST


def one_axis_at_a_time(shard, axes):
    return functools.reduce(lax.psum, axes, shard)


def from_everyone(shard, axis):
    devices = lax.axis_size(axis)
    return lax.all_to_all(
        jnp.broadcast_to(shard[None], (devices, *shard.shape)), axis, 0, 0, tiled=True
    )


def laid_out(pieces, dim):
    pieces = jnp.moveaxis(pieces, 0, dim)
    dims = pieces.shape
    return pieces.reshape(*dims[:dim], dims[dim] * dims[dim + 1], *dims[dim + 2 :])


def gathered_copies(shard, axis, dim):
    pieces = from_everyone(shard, axis)
    return laid_out(pieces, dim)


def steering_table(beam_entries):
    element_index = jnp.arange(ARRAY_ELEMENTS, dtype=jnp.int32)
    steer_phases = (beam_entries[..., None] * element_index % ARRAY_ELEMENTS).astype(
        jnp.float32
    ) * (2.0 * math.pi / ARRAY_ELEMENTS)
    return jnp.stack([jnp.cos(steer_phases), jnp.sin(steer_phases)], axis=-2)


def orthonormal(vectors):
    dims_in = vectors.shape
    flattened = vectors.reshape(dims_in[:-2] + (dims_in[-2] * dims_in[-1],))
    gram_matrix = jnp.einsum("...kx,...lx->...kl", flattened, flattened, precision=highest)
    factor = jnp.linalg.cholesky(gram_matrix)
    solved = lax.linalg.triangular_solve(factor, flattened, left_side=True, lower=True)
    return solved.reshape(dims_in)


def apply_rows(covariance, vectors):
    upper_half = vectors[..., 0, :]
    lower_half = vectors[..., 1, :]
    stacked = jnp.stack(
        [jnp.stack([upper_half, -lower_half], -2), jnp.stack([lower_half, upper_half], -2)], -3
    )
    return jnp.einsum("...bhpa,...pra->...bhr", stacked, covariance, precision=highest)


def project(vectors, subspace):
    coefficients = jnp.einsum("...bha,...kha->...bk", vectors, subspace, precision=highest)
    return vectors - jnp.einsum("...bk,...kha->...bha", coefficients, subspace, precision=highest)


def shards(voltages, rfi_flags, beam_steer_index, start_columns):
    turned = lax.all_to_all(voltages, "chan", split_axis=0, concat_axis=3, tiled=True)
    tile_total_count = lax.axis_size(TILE)
    block_row_set = ARRAY_ELEMENTS // tile_total_count
    first_row = lax.axis_index(TILE) * block_row_set
    gathered = lax.all_gather(turned, TILE, axis=2, tiled=True)
    own_rows = lax.dynamic_slice_in_dim(gathered, first_row, block_row_set, 3)
    swapped = jnp.stack([own_rows[:, 1], -own_rows[:, 0]], 1)
    real_part = jnp.einsum("cpsi,cpsj->cij", own_rows, gathered, preferred_element_type=jnp.float32)
    imag_part = jnp.einsum("cpsi,cpsj->cij", swapped, gathered, preferred_element_type=jnp.float32)
    summed = jnp.stack([real_part, imag_part], 1)
    covariance = summed * (1.0 / SNAPSHOT_COUNT)
    diagonal = lax.dynamic_slice_in_dim(covariance[:, 0], first_row, block_row_set, 2)
    covariance_trace = one_axis_at_a_time(
        jnp.sum(jnp.diagonal(diagonal, axis1=1, axis2=2), axis=1), TILE
    )
    loading_amount = diagonal_loading * covariance_trace / ARRAY_ELEMENTS
    picked = jnp.take_along_axis(covariance, start_columns[:, None, None, :], axis=3)
    col_real = jnp.swapaxes(picked[:, 0], 1, 2)
    col_imag = jnp.swapaxes(picked[:, 1], 1, 2)
    rows_now = jnp.concatenate(
        [jnp.stack([col_real, col_imag], 2), jnp.stack([-col_imag, col_real], 2)], 1
    )
    for sweep_index in range(SUB_ITERS):
        full_rows = gathered_copies(rows_now, TILE, 3)
        subspace = orthonormal(full_rows)
        if sweep_index + 1 < SUB_ITERS:
            rows_now = apply_rows(covariance, subspace)
    subspace = subspace * rfi_flags.astype(jnp.float32)[:, None, None, None]
    steering = steering_table(beam_steer_index)
    load_wide = loading_amount[:, None, None, None]
    load_narrow = loading_amount[:, None]

    def cg_sweep(counter, state_tuple):
        solved_weights, residual, direction, res_norm = state_tuple
        projected = project(direction, subspace)
        mapped = gathered_copies(apply_rows(covariance, projected), TILE, 3)
        combined = project(mapped, subspace) + load_wide * direction
        curvature = jnp.sum(projected * mapped, axis=(2, 3)) + load_narrow * jnp.sum(
            direction * direction, axis=(2, 3)
        )
        step_size = res_norm / curvature
        solved_weights = solved_weights + step_size[:, :, None, None] * direction
        residual = residual - step_size[:, :, None, None] * combined
        new_norm = jnp.sum(residual * residual, axis=(2, 3))
        direction = residual + (new_norm / res_norm)[:, :, None, None] * direction
        return (solved_weights, residual, direction, new_norm)

    start_state = (
        jnp.zeros_like(steering),
        steering,
        steering,
        jnp.sum(steering * steering, axis=(2, 3)),
    )
    solved_weights = lax.fori_loop(0, CG_ITERS, cg_sweep, start_state)[0]
    array_response = jnp.sum(steering * solved_weights, axis=(2, 3))
    weights = ARRAY_ELEMENTS * solved_weights / array_response[:, :, None, None]
    shard_local_rows = lax.dynamic_slice_in_dim(weights, first_row, block_row_set, 3)
    return (covariance, shard_local_rows)


def solution(mesh):
    split = Mesh(mesh.devices.reshape(mesh.shape["chan"], 4, 4), ("chan", "tile_0", "tile_1"))
    return jax.shard_map(
        shards,
        mesh=split,
        in_specs=(P(None, None, TILE, "chan"), P("chan"), P("chan", None), P("chan", None)),
        out_specs=(P("chan", None, TILE, None), P("chan", None, None, TILE)),
        check_vma=False,
    )
```

profile of v0, /device:TPU:0, one launch (start us, length us, event | category | flops | bytes accessed | tf_op | source)
XLA Modules:
  0.0 600.0 jit_solution(14355733121557029052)
XLA Ops:
  7.2 20.4 %all_to_all.45 = bf16[8,2,128,256]{3,2,1,0:T(8,128)(2,1)S(1)} all-to-all(bf16[8,2,128,256]{3,2,1,0:T(8,128)(2,1)} %param.9), channel_id=1, replica_groups=mesh['chan'=8,'tile_0'=4,'tile_1'=4] {'chan'}, dimensions={0} | all-to-all | bytes 2097152 | tf_op jit(solution)/shard_map/all_to_all | solution.py:75
  28.8 112.0 %all-gather.2.cloned.1.call-done = bf16[1,2,2048,2048]{3,2,1,0:T(8,128)(2,1)} async-done(((bf16[1,2,128,2048]{3,2,1,0:T(8,128)(2,1)}), bf16[1,2,2048,2048]{3,2,1,0:T(8,128)(2,1)}) %all-gather.2.cloned.1.call-update) | async-done | bytes 16777232 | tf_op jit(solution)/shard_map/all_gather | solution.py:79
  140.7 8.6 %fusion.26 = f32[128,2048,1]{1,0,2:T(8,128)S(1)} fusion(bf16[1,2,2048,2048]{3,2,1,0:T(8,128)(2,1)} %all-gather.2.cloned.1.call-done, s32[]{:T(128)S(6)} %select_n.91), kind=kOutput, calls=%fused_computation.39 | convolution fusion | flops 2147483648 | bytes 18874372 | tf_op jit(solution)/shard_map/cpsi,cpsj->cij/dot_general | solution.py:82
  155.8 4.1 copy.86
  162.4 22.4 %all_to_all.46 = f32[16,1,64,2,128]{4,2,3,1,0:T(8,128)S(1)} all-to-all(f32[16,1,64,2,128]{4,2,3,1,0:T(8,128)S(1)} %broadcast_in_dim.49), channel_id=1, replica_groups=mesh['chan'=8,'tile_0'=4,'tile_1'=4] {'tile_0','tile_1'}, dimensions={0} | all-to-all | bytes 2097152 | tf_op jit(solution)/shard_map/all_to_all | solution.py:27
  185.8 5.8 custom-call.15
  193.0 4.9 custom-call.16
  198.6 2.6 convolution_bitcast_fusion.4
  206.7 19.7 %all_to_all.47 = f32[16,1,64,2,128]{4,2,3,1,0:T(8,128)S(1)} all-to-all(f32[16,1,64,2,128]{4,2,3,1,0:T(8,128)S(1)} %broadcast_in_dim.74), channel_id=1, replica_groups=mesh['chan'=8,'tile_0'=4,'tile_1'=4] {'tile_0','tile_1'}, dimensions={0} | all-to-all | bytes 2097152 | tf_op jit(solution)/shard_map/all_to_all | solution.py:27
  227.5 5.8 custom-call.17
  234.7 4.9 custom-call.18
  240.3 2.6 convolution_bitcast_fusion.3
  249.5 3.8 all-to-all-start.4
  254.5 14.5 %all-to-all-done.4 = f32[16,1,64,2,128]{4,2,3,1,0:T(8,128)S(1)} async-done(((f32[16,1,64,2,128]{4,2,3,1,0:T(8,128)}), f32[16,1,64,2,128]{4,2,3,1,0:T(8,128)S(1)}, u32[]{:S(2)}, u32[]{:S(2)}) %all-to-all-start.4) | async-done | bytes 1048608 | tf_op jit(solution)/shard_map/all_to_all | solution.py:27
  270.0 5.8 custom-call.19
  277.2 4.9 custom-call.20
  282.8 2.6 convolution_bitcast_fusion.2
  291.9 4.3 all-to-all-start.5
  300.7 11.9 %psum.14 = f32[1]{0:T(128)} all-reduce(f32[1]{0:T(128)} %bitcast.91), channel_id=1, replica_groups=mesh['chan'=8,'tile_0'=4,'tile_1'=4] {'tile_0'}, use_global_device_ids=true, to_apply=%region_4.7 | all-reduce | flops 1 | bytes 8 | tf_op jit(solution)/shard_map/psum | solution.py:22
  313.5 10.8 %psum.15 = f32[1]{0:T(128)} all-reduce(f32[1]{0:T(128)} %psum.14), channel_id=1, replica_groups=mesh['chan'=8,'tile_0'=4,'tile_1'=4] {'tile_1'}, use_global_device_ids=true, to_apply=%region_5.8 | all-reduce | flops 1 | bytes 8 | tf_op jit(solution)/shard_map/psum | solution.py:22
  325.0 2.5 fusion.55
  327.6 5.8 custom-call.21
  334.8 4.9 custom-call.22
  343.3 246.5 %while.17 = (s32[]{:T(128)}, f32[1,8,2,2048]{3,1,2,0:T(8,128)}, f32[1,8,2,2048]{3,1,2,0:T(8,128)}, f32[1,8,2,2048]{3,1,2,0:T(8,128)S(1)}, f32[1,8]{1,0:T(1,128)S...) while((s32[]{:T(128)}, f32[1,8,2,2048]{3,1,2,0:T(8,128)}, ...), condition=%wide.region_10.13_spmd.clone, body=%wide.region_6.12_spmd.clone.sunk | while | flops 202031136 | bytes 11035319 | solution.py:128
  347.3 3.5 all-to-all-start
  351.0 7.8 %all-to-all-done = f32[16,1,8,2,128]{4,2,3,1,0:T(8,128)S(1)} async-done(((f32[16,1,8,2,128]{4,2,3,1,0:T(8,128)}), f32[16,1,8,2,128]{4,2,3,1,0:T(8,128)S(1)}, u32[]{:S(2)}, u32[]{:S(2)}) %all-to-all-start) | async-done | bytes 131104 | tf_op jit(solution)/shard_map/while/body/eval_jaxpr/all_to_all | solution.py:27
  367.9 3.5 all-to-all-start
  371.6 7.8 %all-to-all-done = f32[16,1,8,2,128]{4,2,3,1,0:T(8,128)S(1)} async-done(((f32[16,1,8,2,128]{4,2,3,1,0:T(8,128)}), f32[16,1,8,2,128]{4,2,3,1,0:T(8,128)S(1)}, u32[]{:S(2)}, u32[]{:S(2)}) %all-to-all-start) | async-done | bytes 131104 | tf_op jit(solution)/shard_map/while/body/eval_jaxpr/all_to_all | solution.py:27
  388.4 3.5 all-to-all-start
  392.1 7.8 %all-to-all-done = f32[16,1,8,2,128]{4,2,3,1,0:T(8,128)S(1)} async-done(((f32[16,1,8,2,128]{4,2,3,1,0:T(8,128)}), f32[16,1,8,2,128]{4,2,3,1,0:T(8,128)S(1)}, u32[]{:S(2)}, u32[]{:S(2)}) %all-to-all-start) | async-done | bytes 131104 | tf_op jit(solution)/shard_map/while/body/eval_jaxpr/all_to_all | solution.py:27
  409.0 3.5 all-to-all-start
  412.6 7.8 %all-to-all-done = f32[16,1,8,2,128]{4,2,3,1,0:T(8,128)S(1)} async-done(((f32[16,1,8,2,128]{4,2,3,1,0:T(8,128)}), f32[16,1,8,2,128]{4,2,3,1,0:T(8,128)S(1)}, u32[]{:S(2)}, u32[]{:S(2)}) %all-to-all-start) | async-done | bytes 131104 | tf_op jit(solution)/shard_map/while/body/eval_jaxpr/all_to_all | solution.py:27
  429.5 3.5 all-to-all-start
  433.2 7.8 %all-to-all-done = f32[16,1,8,2,128]{4,2,3,1,0:T(8,128)S(1)} async-done(((f32[16,1,8,2,128]{4,2,3,1,0:T(8,128)}), f32[16,1,8,2,128]{4,2,3,1,0:T(8,128)S(1)}, u32[]{:S(2)}, u32[]{:S(2)}) %all-to-all-start) | async-done | bytes 131104 | tf_op jit(solution)/shard_map/while/body/eval_jaxpr/all_to_all | solution.py:27
  450.0 3.5 all-to-all-start
  453.7 7.8 %all-to-all-done = f32[16,1,8,2,128]{4,2,3,1,0:T(8,128)S(1)} async-done(((f32[16,1,8,2,128]{4,2,3,1,0:T(8,128)}), f32[16,1,8,2,128]{4,2,3,1,0:T(8,128)S(1)}, u32[]{:S(2)}, u32[]{:S(2)}) %all-to-all-start) | async-done | bytes 131104 | tf_op jit(solution)/shard_map/while/body/eval_jaxpr/all_to_all | solution.py:27
  470.6 3.5 all-to-all-start
  474.3 7.8 %all-to-all-done = f32[16,1,8,2,128]{4,2,3,1,0:T(8,128)S(1)} async-done(((f32[16,1,8,2,128]{4,2,3,1,0:T(8,128)}), f32[16,1,8,2,128]{4,2,3,1,0:T(8,128)S(1)}, u32[]{:S(2)}, u32[]{:S(2)}) %all-to-all-start) | async-done | bytes 131104 | tf_op jit(solution)/shard_map/while/body/eval_jaxpr/all_to_all | solution.py:27
  491.1 3.5 all-to-all-start
  494.8 7.8 %all-to-all-done = f32[16,1,8,2,128]{4,2,3,1,0:T(8,128)S(1)} async-done(((f32[16,1,8,2,128]{4,2,3,1,0:T(8,128)}), f32[16,1,8,2,128]{4,2,3,1,0:T(8,128)S(1)}, u32[]{:S(2)}, u32[]{:S(2)}) %all-to-all-start) | async-done | bytes 131104 | tf_op jit(solution)/shard_map/while/body/eval_jaxpr/all_to_all | solution.py:27
  511.7 3.5 all-to-all-start
  515.3 7.8 %all-to-all-done = f32[16,1,8,2,128]{4,2,3,1,0:T(8,128)S(1)} async-done(((f32[16,1,8,2,128]{4,2,3,1,0:T(8,128)}), f32[16,1,8,2,128]{4,2,3,1,0:T(8,128)S(1)}, u32[]{:S(2)}, u32[]{:S(2)}) %all-to-all-start) | async-done | bytes 131104 | tf_op jit(solution)/shard_map/while/body/eval_jaxpr/all_to_all | solution.py:27
  532.2 3.5 all-to-all-start
  535.9 7.8 %all-to-all-done = f32[16,1,8,2,128]{4,2,3,1,0:T(8,128)S(1)} async-done(((f32[16,1,8,2,128]{4,2,3,1,0:T(8,128)}), f32[16,1,8,2,128]{4,2,3,1,0:T(8,128)S(1)}, u32[]{:S(2)}, u32[]{:S(2)}) %all-to-all-start) | async-done | bytes 131104 | tf_op jit(solution)/shard_map/while/body/eval_jaxpr/all_to_all | solution.py:27
  552.7 3.5 all-to-all-start
  556.4 7.8 %all-to-all-done = f32[16,1,8,2,128]{4,2,3,1,0:T(8,128)S(1)} async-done(((f32[16,1,8,2,128]{4,2,3,1,0:T(8,128)}), f32[16,1,8,2,128]{4,2,3,1,0:T(8,128)S(1)}, u32[]{:S(2)}, u32[]{:S(2)}) %all-to-all-start) | async-done | bytes 131104 | tf_op jit(solution)/shard_map/while/body/eval_jaxpr/all_to_all | solution.py:27
  573.3 3.5 all-to-all-start
  577.0 7.8 %all-to-all-done = f32[16,1,8,2,128]{4,2,3,1,0:T(8,128)S(1)} async-done(((f32[16,1,8,2,128]{4,2,3,1,0:T(8,128)}), f32[16,1,8,2,128]{4,2,3,1,0:T(8,128)S(1)}, u32[]{:S(2)}, u32[]{:S(2)}) %all-to-all-start) | async-done | bytes 131104 | tf_op jit(solution)/shard_map/while/body/eval_jaxpr/all_to_all | solution.py:27
  (315 shorter events, 161.5 us)
Async XLA Ops:
  7.2 133.6 %all-gather.2.cloned.1.call-start = ((), (), s32[]{:S(2)}) async-start(), calls=%async_computation.6 | async-start | bytes 17825792 | tf_op jit(solution)/shard_map/all_gather | solution.py:79
  27.6 1.1 copy-start.8
  140.7 10.9 %copy-start = (bf16[1,2,2048,2048]{3,2,1,0:T(8,128)(2,1)S(1)}, bf16[1,2,2048,2048]{3,2,1,0:T(8,128)(2,1)}, u32[]{:S(2)}) copy-start(bf16[1,2,2048,2048]{3,2,1,0:T(8,128)(2,1)} %all-gather.2.cloned.1.call-done) | copy-start | bytes 50331652
  151.6 137.2 %copy-start.2 = (f32[128,2048,1]{1,0,2:T(8,128)}, f32[128,2048,1]{1,0,2:T(8,128)S(1)}, u32[]{:S(2)}) copy-start(f32[128,2048,1]{1,0,2:T(8,128)S(1)} %fusion.26) | copy-start | bytes 3145732
  248.4 5.6 copy-start.7
  249.5 19.5 %all-to-all-start.4 = ((f32[16,1,64,2,128]{4,2,3,1,0:T(8,128)}), f32[16,1,64,2,128]{4,2,3,1,0:T(8,128)S(1)}, u32[]{:S(2)}, u32[]{:S(2)}) async-start(f32[16,1,64,2,128]{4,2,3,1,0:T(8,128)} %broadcast_in_dim.75), calls=%async_computation.4 | async-start | bytes 2097152 | tf_op jit(solution)/shard_map/all_to_all | solution.py:27
  291.9 33.1 %all-to-all-start.5 = ((f32[16,1,64,2,128]{4,2,3,1,0:T(8,128)}), f32[16,1,64,2,128]{4,2,3,1,0:T(8,128)}, u32[]{:S(2)}, u32[]{:S(2)}) async-start(f32[16,1,64,2,128]{4,2,3,1,0:T(8,128)} %broadcast_in_dim.76), calls=%async_computation.5 | async-start | bytes 2097152 | tf_op jit(solution)/shard_map/all_to_all | solution.py:27
  296.6 0.7 copy-start.5
  296.6 2.1 copy-start.6
  347.3 11.5 %all-to-all-start = ((f32[16,1,8,2,128]{4,2,3,1,0:T(8,128)}), f32[16,1,8,2,128]{4,2,3,1,0:T(8,128)S(1)}, u32[]{:S(2)}, u32[]{:S(2)}) async-start(f32[16,1,8,2,128]{4,2,3,1,0:T(8,128)} %broadcast_in_dim.83), calls=%async_computation | async-start | bytes 262144 | tf_op jit(solution)/shard_map/while/body/eval_jaxpr/all_to_all | solution.py:27
  358.8 3.4 copy-start.3
  363.2 0.6 copy-start.4
  367.9 11.5 %all-to-all-start = ((f32[16,1,8,2,128]{4,2,3,1,0:T(8,128)}), f32[16,1,8,2,128]{4,2,3,1,0:T(8,128)S(1)}, u32[]{:S(2)}, u32[]{:S(2)}) async-start(f32[16,1,8,2,128]{4,2,3,1,0:T(8,128)} %broadcast_in_dim.83), calls=%async_computation | async-start | bytes 262144 | tf_op jit(solution)/shard_map/while/body/eval_jaxpr/all_to_all | solution.py:27
  379.4 3.4 copy-start.3
  383.8 0.6 copy-start.4
  388.4 11.5 %all-to-all-start = ((f32[16,1,8,2,128]{4,2,3,1,0:T(8,128)}), f32[16,1,8,2,128]{4,2,3,1,0:T(8,128)S(1)}, u32[]{:S(2)}, u32[]{:S(2)}) async-start(f32[16,1,8,2,128]{4,2,3,1,0:T(8,128)} %broadcast_in_dim.83), calls=%async_computation | async-start | bytes 262144 | tf_op jit(solution)/shard_map/while/body/eval_jaxpr/all_to_all | solution.py:27
  399.9 3.4 copy-start.3
  404.3 0.6 copy-start.4
  409.0 11.5 %all-to-all-start = ((f32[16,1,8,2,128]{4,2,3,1,0:T(8,128)}), f32[16,1,8,2,128]{4,2,3,1,0:T(8,128)S(1)}, u32[]{:S(2)}, u32[]{:S(2)}) async-start(f32[16,1,8,2,128]{4,2,3,1,0:T(8,128)} %broadcast_in_dim.83), calls=%async_computation | async-start | bytes 262144 | tf_op jit(solution)/shard_map/while/body/eval_jaxpr/all_to_all | solution.py:27
  420.4 3.4 copy-start.3
  424.9 0.6 copy-start.4
  429.5 11.5 %all-to-all-start = ((f32[16,1,8,2,128]{4,2,3,1,0:T(8,128)}), f32[16,1,8,2,128]{4,2,3,1,0:T(8,128)S(1)}, u32[]{:S(2)}, u32[]{:S(2)}) async-start(f32[16,1,8,2,128]{4,2,3,1,0:T(8,128)} %broadcast_in_dim.83), calls=%async_computation | async-start | bytes 262144 | tf_op jit(solution)/shard_map/while/body/eval_jaxpr/all_to_all | solution.py:27
  441.0 3.4 copy-start.3
  445.4 0.6 copy-start.4
  450.0 11.5 %all-to-all-start = ((f32[16,1,8,2,128]{4,2,3,1,0:T(8,128)}), f32[16,1,8,2,128]{4,2,3,1,0:T(8,128)S(1)}, u32[]{:S(2)}, u32[]{:S(2)}) async-start(f32[16,1,8,2,128]{4,2,3,1,0:T(8,128)} %broadcast_in_dim.83), calls=%async_computation | async-start | bytes 262144 | tf_op jit(solution)/shard_map/while/body/eval_jaxpr/all_to_all | solution.py:27
  461.5 3.4 copy-start.3
  465.9 0.6 copy-start.4
  470.6 11.5 %all-to-all-start = ((f32[16,1,8,2,128]{4,2,3,1,0:T(8,128)}), f32[16,1,8,2,128]{4,2,3,1,0:T(8,128)S(1)}, u32[]{:S(2)}, u32[]{:S(2)}) async-start(f32[16,1,8,2,128]{4,2,3,1,0:T(8,128)} %broadcast_in_dim.83), calls=%async_computation | async-start | bytes 262144 | tf_op jit(solution)/shard_map/while/body/eval_jaxpr/all_to_all | solution.py:27
  482.1 3.4 copy-start.3
  486.5 0.6 copy-start.4
  491.1 11.5 %all-to-all-start = ((f32[16,1,8,2,128]{4,2,3,1,0:T(8,128)}), f32[16,1,8,2,128]{4,2,3,1,0:T(8,128)S(1)}, u32[]{:S(2)}, u32[]{:S(2)}) async-start(f32[16,1,8,2,128]{4,2,3,1,0:T(8,128)} %broadcast_in_dim.83), calls=%async_computation | async-start | bytes 262144 | tf_op jit(solution)/shard_map/while/body/eval_jaxpr/all_to_all | solution.py:27
  502.6 3.4 copy-start.3
  507.0 0.6 copy-start.4
  511.7 11.5 %all-to-all-start = ((f32[16,1,8,2,128]{4,2,3,1,0:T(8,128)}), f32[16,1,8,2,128]{4,2,3,1,0:T(8,128)S(1)}, u32[]{:S(2)}, u32[]{:S(2)}) async-start(f32[16,1,8,2,128]{4,2,3,1,0:T(8,128)} %broadcast_in_dim.83), calls=%async_computation | async-start | bytes 262144 | tf_op jit(solution)/shard_map/while/body/eval_jaxpr/all_to_all | solution.py:27
  523.1 3.4 copy-start.3
  527.6 0.6 copy-start.4
  532.2 11.5 %all-to-all-start = ((f32[16,1,8,2,128]{4,2,3,1,0:T(8,128)}), f32[16,1,8,2,128]{4,2,3,1,0:T(8,128)S(1)}, u32[]{:S(2)}, u32[]{:S(2)}) async-start(f32[16,1,8,2,128]{4,2,3,1,0:T(8,128)} %broadcast_in_dim.83), calls=%async_computation | async-start | bytes 262144 | tf_op jit(solution)/shard_map/while/body/eval_jaxpr/all_to_all | solution.py:27
  543.7 3.4 copy-start.3
  548.1 0.6 copy-start.4
  552.7 11.5 %all-to-all-start = ((f32[16,1,8,2,128]{4,2,3,1,0:T(8,128)}), f32[16,1,8,2,128]{4,2,3,1,0:T(8,128)S(1)}, u32[]{:S(2)}, u32[]{:S(2)}) async-start(f32[16,1,8,2,128]{4,2,3,1,0:T(8,128)} %broadcast_in_dim.83), calls=%async_computation | async-start | bytes 262144 | tf_op jit(solution)/shard_map/while/body/eval_jaxpr/all_to_all | solution.py:27
  564.2 3.4 copy-start.3
  568.6 0.6 copy-start.4
  573.3 11.5 %all-to-all-start = ((f32[16,1,8,2,128]{4,2,3,1,0:T(8,128)}), f32[16,1,8,2,128]{4,2,3,1,0:T(8,128)S(1)}, u32[]{:S(2)}, u32[]{:S(2)}) async-start(f32[16,1,8,2,128]{4,2,3,1,0:T(8,128)} %broadcast_in_dim.83), calls=%async_computation | async-start | bytes 262144 | tf_op jit(solution)/shard_map/while/body/eval_jaxpr/all_to_all | solution.py:27
  584.8 3.4 copy-start.3
  589.2 0.6 copy-start.4
  589.8 3.1 copy-start.1
Sparse Core Ops, SparseCore 0:
  28.9 111.8 all-gather.1
where the time goes:
time: 607 us; the launch traced here: 600 us
  waiting for transfers between devices  220 us (36%)
  matrix products  109 us (18%)
  blocking collectives  85.2 us (14%)
  other arithmetic  73.4 us (12%)
  starting transfers between devices  50.4 us (8%)
  local copies, waits for them, and re-layouts  45 us (7%)
  between operations  16.1 us (3%)
    all_gather x1, waiting for transfers between devices, shards(): gathered = lax.all_gather(turned, TILE, axis=2, tiled=True)  112 us
    all_to_all x14, waiting for transfers between devices, from_everyone(): lax.all_to_all(jnp.broadcast_to(shard[None], (devices, *shard.shape)), ax...  108 us
    all_to_all x14, starting transfers between devices, from_everyone(): lax.all_to_all(jnp.broadcast_to(shard[None], (devices, *shard.shape)), ax...  50.3 us
    all_to_all x2, blocking collectives, from_everyone(): lax.all_to_all(jnp.broadcast_to(shard[None], (devices, *shard.shape)), ax...  42.1 us
    dot_general x24, matrix products, project(): jnp.einsum('...bk,...kha->...bha', coefficients, subspace, precision=high...  35 us
    dot_general x15, matrix products, apply_rows(): jnp.einsum('...bhpa,...pra->...bhr', stacked, covariance, precision=highest)  26.4 us
    another operation x12, other arithmetic, orthonormal(): factor = jnp.linalg.cholesky(gram_matrix)  26.1 us
    psum x2, blocking collectives, one_axis_at_a_time(): return functools.reduce(lax.psum, axes, shard)  22.7 us
  transfers between devices with their start and end apart: 15, of which 14 were waited for; matrix products, arithmetic and copies ran while one was open for 1% of the time, Pallas kernels for 0%

commit v1 on v0

v1 whole, which is shorter than its diff:
```python
import functools
import math

import jax
import jax.numpy as jnp
from jax import lax
from jax.experimental import pallas as pl
from jax.experimental.pallas import tpu as pltpu
from jax.sharding import Mesh
from jax.sharding import PartitionSpec as P

ARRAY_ELEMENTS = 2048
SNAPSHOT_COUNT = 2048
SUBSPACE_SIZE = 32
BEAM_COUNT = 8
SUB_ITERS = 4
CG_ITERS = 12
TILE = ("tile_0", "tile_1")
TILES = 16
ROWS = 128
WIDE = 256

diagonal_loading = 0.1
highest = lax.Precision.HIGHEST
f32 = jnp.float32
bf16 = jnp.bfloat16


def pieces(x):
    hi = x.astype(bf16)
    rest = x - hi.astype(f32)
    mid = rest.astype(bf16)
    low = (rest - mid.astype(f32)).astype(bf16)
    return jnp.concatenate([hi, mid, low], 0)


def fold(x, count):
    rows = x.shape[0] // count
    total = x[:rows]
    for n in range(1, count):
        total = total + x[n * rows : (n + 1) * rows]
    return total


def plain(a, b):
    return lax.dot_general(a, b, (((1,), (0,)), ((), ())), preferred_element_type=f32)


def turned_dot(a, b, precision=None):
    return lax.dot_general(
        a, b, (((1,), (1,)), ((), ())), preferred_element_type=f32, precision=precision
    )


def through(lhs, matrix, count, sign):
    parts = []
    for n in range(ARRAY_ELEMENTS // WIDE):
        cols = pl.ds(n * WIDE, WIDE)
        by_real = fold(plain(lhs[...], matrix[0, :, cols]), count)
        by_imag = fold(plain(lhs[...], matrix[1, :, cols]), count)
        half = by_real.shape[0] // 2
        swapped = jnp.concatenate([-by_imag[half:], by_imag[:half]], 0)
        parts.append(by_real + swapped if sign > 0 else by_real - swapped)
    return jnp.concatenate(parts, 1)


def beam_sum(x):
    folded = x[:BEAM_COUNT] + x[BEAM_COUNT:]
    return jnp.sum(folded, axis=1, keepdims=True)


def twice(x):
    return jnp.concatenate([x, x], 0)


def unit_rows(y):
    size = SUBSPACE_SIZE
    y_real, y_imag = y[:size], y[size:]
    crossed = jnp.concatenate([y_imag, -y_real], 0)
    gram = turned_dot(y, y_real, highest) + turned_dot(crossed, y_imag, highest)
    a_r, a_i = gram[:size], gram[size:]
    row = lax.broadcasted_iota(jnp.int32, (size, size), 0)
    col = lax.broadcasted_iota(jnp.int32, (size, size), 1)
    j_r = jnp.where(row == col, 1.0, 0.0).astype(f32)
    j_i = jnp.zeros((size, size), f32)
    for k in range(size - 1):
        below = row[:, :1] > k
        inverse = 1.0 / a_r[k : k + 1, k : k + 1]
        f_r = jnp.where(below, a_r[:, k : k + 1] * inverse, 0.0)
        f_i = jnp.where(below, a_i[:, k : k + 1] * inverse, 0.0)
        p_r, p_i = a_r[k : k + 1], a_i[k : k + 1]
        q_r, q_i = j_r[k : k + 1], j_i[k : k + 1]
        a_r, a_i = a_r - (f_r * p_r - f_i * p_i), a_i - (f_r * p_i + f_i * p_r)
        j_r, j_i = j_r - (f_r * q_r - f_i * q_i), j_i - (f_r * q_i + f_i * q_r)
    pivots = jnp.sum(jnp.where(row == col, a_r, 0.0), axis=1, keepdims=True)
    scale = 1.0 / jnp.sqrt(pivots)
    j_r, j_i = j_r * scale, j_i * scale
    by_real = jnp.concatenate([j_r, j_i], 0)
    by_imag = jnp.concatenate([-j_i, j_r], 0)
    return lax.dot_general(
        by_real, y_real, (((1,), (0,)), ((), ())), preferred_element_type=f32, precision=highest
    ) + lax.dot_general(
        by_imag, y_imag, (((1,), (0,)), ((), ())), preferred_element_type=f32, precision=highest
    )


def weights_kernel(
    flag, place, voltages, picks, steering, out, v, vt, basis, basis_t, wide, narrow, spread, state, sems
):
    inverse_count = 1.0 / SNAPSHOT_COUNT

    def copy(n, part):
        rows = pl.ds(n * ROWS, ROWS)
        return pltpu.make_async_copy(voltages.at[n, part], v.at[part, rows], sems.at[n, part])

    for n in range(TILES):
        for part in range(2):
            copy(n, part).start()

    squares = jnp.zeros((8, ARRAY_ELEMENTS), f32)
    for n in range(TILES):
        for part in range(2):
            copy(n, part).wait()
            block = v[part, n * ROWS : (n + 1) * ROWS, :]
            vt[part, :, n * ROWS : (n + 1) * ROWS] = block.T
            exact = block.astype(f32)
            squares = squares + jnp.sum((exact * exact).reshape(ROWS // 8, 8, ARRAY_ELEMENTS), axis=0)
    power = jnp.sum(jnp.sum(squares, axis=0, keepdims=True), axis=1, keepdims=True)
    load = diagonal_loading * (power * inverse_count) / ARRAY_ELEMENTS

    for n in range(ARRAY_ELEMENTS // WIDE):
        cols = pl.ds(n * WIDE, WIDE)
        taken_r = plain(picks[...], vt[0, :, cols])
        taken_i = plain(picks[...], vt[1, :, cols])
        wide[: 2 * SUBSPACE_SIZE, cols] = jnp.concatenate([taken_r, -taken_i], 0).astype(bf16)
    spread[...] = through(wide.at[: 2 * SUBSPACE_SIZE], v, 1, 1) * inverse_count
    spread[...] = unit_rows(spread[...])

    def sweep(n, carry):
        wide[...] = pieces(spread[...])
        wide[...] = pieces(through(wide, vt, 3, -1))
        spread[...] = through(wide, v, 3, 1) * inverse_count
        spread[...] = unit_rows(spread[...])
        return carry

    lax.fori_loop(0, SUB_ITERS - 1, sweep, 0)
    found = spread[...] * flag[0].astype(f32)
    blank = jnp.zeros((SUBSPACE_SIZE, ARRAY_ELEMENTS), bf16)
    basis[...] = jnp.concatenate(
        [pieces(found[:SUBSPACE_SIZE]), blank, pieces(found[SUBSPACE_SIZE:]), blank], 0
    )
    basis_t[...] = basis[...].T

    def project(x):
        narrow[...] = pieces(x)
        raw = fold(plain(narrow[...], basis_t[...]), 3)
        half = BEAM_COUNT
        c_r = raw[:half, :128] + raw[half:, 128:]
        c_i = raw[half:, :128] - raw[:half, 128:]
        c = jnp.concatenate([c_r, c_i], 0)
        c = c + pltpu.roll(c, 64, 1)
        c = c + pltpu.roll(c, 32, 1)
        c_split = pieces(c)
        d_split = pieces(jnp.concatenate([-c[half:], c[:half]], 0))
        both = jnp.concatenate([c_split, d_split], 1)
        return x - fold(plain(both, basis[...]), 3)

    source = steering[...]
    state[0] = jnp.zeros_like(source)
    clean = project(source)
    state[1] = clean
    state[2] = clean
    state[3] = source - clean
    inside = beam_sum((source - clean) * (source - clean))

    def correlate():
        narrow[...] = pieces(state[2])
        return through(narrow, vt, 3, -1)

    def curvature_of(seen, direction, tau):
        return beam_sum(seen * seen) * inverse_count + load * (
            beam_sum(direction * direction) + tau * tau * inside
        )

    def iterate(n, carry):
        norm, xi, rho, tau = carry
        seen = correlate()
        direction = state[2]
        step = norm / curvature_of(seen, direction, tau)
        narrow[...] = pieces(seen)
        mapped = project(through(narrow, v, 3, 1) * inverse_count) + load * direction
        state[0] = state[0] + twice(step) * direction
        residual = state[1] - twice(step) * mapped
        state[1] = residual
        xi = xi + step * tau
        rho = rho - step * (load * tau)
        fresh = beam_sum(residual * residual) + rho * rho * inside
        ratio = fresh / norm
        state[2] = residual + twice(ratio) * direction
        tau = rho + ratio * tau
        return fresh, xi, rho, tau

    one = jnp.ones((BEAM_COUNT, 1), f32)
    first = (beam_sum(source * source), jnp.zeros((BEAM_COUNT, 1), f32), one, one)
    norm, xi, rho, tau = lax.fori_loop(0, CG_ITERS - 1, iterate, first)
    direction = state[2]
    step = norm / curvature_of(correlate(), direction, tau)
    solved = state[0] + twice(step) * direction + twice(xi + step * tau) * state[3]
    response = beam_sum(source * solved)
    state[0] = ARRAY_ELEMENTS * solved / twice(response)
    out[...] = state[0, :, pl.ds(pl.multiple_of(place[0] * ROWS, ROWS), ROWS)]


def local_weights(flag, place, gathered, picks, steering, interpret=False):
    vmem = pl.BlockSpec(memory_space=pltpu.VMEM)
    smem = pl.BlockSpec(memory_space=pltpu.SMEM)
    return pl.pallas_call(
        weights_kernel,
        out_shape=jax.ShapeDtypeStruct((2 * BEAM_COUNT, ROWS), f32),
        in_specs=[smem, smem, pl.BlockSpec(memory_space=pl.ANY), vmem, vmem],
        out_specs=vmem,
        scratch_shapes=[
            pltpu.VMEM((2, SNAPSHOT_COUNT, ARRAY_ELEMENTS), bf16),
            pltpu.VMEM((2, ARRAY_ELEMENTS, SNAPSHOT_COUNT), bf16),
            pltpu.VMEM((8 * SUBSPACE_SIZE, ARRAY_ELEMENTS), bf16),
            pltpu.VMEM((ARRAY_ELEMENTS, 8 * SUBSPACE_SIZE), bf16),
            pltpu.VMEM((6 * SUBSPACE_SIZE, ARRAY_ELEMENTS), bf16),
            pltpu.VMEM((6 * BEAM_COUNT, ARRAY_ELEMENTS), bf16),
            pltpu.VMEM((2 * SUBSPACE_SIZE, ARRAY_ELEMENTS), f32),
            pltpu.VMEM((4, 2 * BEAM_COUNT, ARRAY_ELEMENTS), f32),
            pltpu.SemaphoreType.DMA((TILES, 2)),
        ],
        compiler_params=pltpu.CompilerParams(vmem_limit_bytes=58 << 20),
        interpret=interpret,
    )(flag, place, gathered, picks, steering)


def steering_table(beam_entries):
    element_index = jnp.arange(ARRAY_ELEMENTS, dtype=jnp.int32)
    steer_phases = (beam_entries[..., None] * element_index % ARRAY_ELEMENTS).astype(f32) * (
        2.0 * math.pi / ARRAY_ELEMENTS
    )
    return jnp.concatenate([jnp.cos(steer_phases), jnp.sin(steer_phases)], axis=0)


def shards(voltages, rfi_flags, beam_steer_index, start_columns):
    turned = lax.all_to_all(voltages, "chan", split_axis=0, concat_axis=3, tiled=True)
    place = lax.axis_index(TILE)
    gathered = lax.all_gather(turned[0], TILE, axis=0, tiled=False)
    own = lax.dynamic_slice_in_dim(gathered, place * ROWS, ROWS, 3)
    swapped = jnp.stack([own[:, 1], -own[:, 0]], 1)
    real_part = jnp.einsum("tpsi,tpsj->ij", own, gathered, preferred_element_type=f32)
    imag_part = jnp.einsum("tpsi,tpsj->ij", swapped, gathered, preferred_element_type=f32)
    covariance = jnp.stack([real_part, imag_part])[None] * (1.0 / SNAPSHOT_COUNT)
    picks = (start_columns[0][:, None] == jnp.arange(ARRAY_ELEMENTS, dtype=jnp.int32)).astype(bf16)
    steering = steering_table(beam_steer_index[0])
    weights = local_weights(rfi_flags, place[None].astype(jnp.int32), gathered, picks, steering)
    weights = jnp.swapaxes(weights.reshape(1, 2, BEAM_COUNT, ROWS), 1, 2)
    return (covariance, weights)


def solution(mesh):
    split = Mesh(mesh.devices.reshape(mesh.shape["chan"], 4, 4), ("chan", "tile_0", "tile_1"))
    return jax.shard_map(
        shards,
        mesh=split,
        in_specs=(P(None, None, TILE, "chan"), P("chan"), P("chan", None), P("chan", None)),
        out_specs=(P("chan", None, TILE, None), P("chan", None, None, TILE)),
        check_vma=False,
    )
```

time: 607 us -> 302 us (0.50)
  Pallas kernels: 0 us -> 134 us
  waiting for transfers between devices: 220 us -> 108 us
  matrix products: 109 us -> 11.1 us
  other arithmetic: 73.4 us -> 5.45 us
  blocking collectives: 85.2 us -> 20.4 us
  starting transfers between devices: 50.4 us -> 0.04 us
  local copies, waits for them, and re-layouts: 45 us -> 6.75 us
    pallas_call x0 -> x1, Pallas kernels: none -> 134 us  [local_weights(): pl.pallas_call(weights_kernel, out_shape=jax.ShapeDtypeStruct((2 * BEAM_C...]
    all_to_all x14 -> x0, waiting for transfers between devices: 108 us -> none  [from_everyone(): lax.all_to_all(jnp.broadcast_to(shard[None], (devices, *shard.shape)), ax...]
    dot_general x69 -> x2, matrix products: 99.7 us -> 11.1 us  [the longest x1 7.68 us: shards(): jnp.einsum('tpsi,tpsj->ij', own, gathered, preferred_element_type=f32)]
    all_to_all x14 -> x0, starting transfers between devices: 50.3 us -> none  [from_everyone(): lax.all_to_all(jnp.broadcast_to(shard[None], (devices, *shard.shape)), ax...]
    another operation x38 -> x0, other arithmetic: 50.2 us -> none  [the longest x12 26.1 us: orthonormal(): factor = jnp.linalg.cholesky(gram_matrix)]
    all_to_all x2 -> x0, blocking collectives: 42.1 us -> none  [from_everyone(): lax.all_to_all(jnp.broadcast_to(shard[None], (devices, *shard.shape)), ax...]
    psum x2 -> x0, blocking collectives: 22.7 us -> none  [one_axis_at_a_time(): return functools.reduce(lax.psum, axes, shard)]
    add x12 -> x0, other arithmetic: 12.3 us -> none  [cg_sweep(): direction = residual + (new_norm / res_norm)[:, :, None, None] * direction]
  transfers between devices with their start and end apart: 15 -> 1, of which waited for: 14 -> 1; matrix products, arithmetic and copies ran while one was open for 1% -> 1% of each run, Pallas kernels for 0% -> 0%
where the time goes in v1:
time: 302 us; the launch traced here: 301 us
  Pallas kernels  134 us (44%)
  waiting for transfers between devices  108 us (36%)
  blocking collectives  20.4 us (7%)
  between operations  14.7 us (5%)
  matrix products  11.1 us (4%)
  local copies, waits for them, and re-layouts  6.75 us (2%)
  other arithmetic  5.45 us (2%)
    pallas_call x1, Pallas kernels, local_weights(): pl.pallas_call(weights_kernel, out_shape=jax.ShapeDtypeStruct((2 * BEAM_C...  134 us
    all_gather x1, waiting for transfers between devices, shards(): gathered = lax.all_gather(turned[0], TILE, axis=0, tiled=False)  108 us
    all_to_all x1, blocking collectives, shards(): lax.all_to_all(voltages, 'chan', split_axis=0, concat_axis=3, tiled=True)  20.4 us
    dot_general x1, matrix products, shards(): jnp.einsum('tpsi,tpsj->ij', own, gathered, preferred_element_type=f32)  7.68 us
  transfers between devices with their start and end apart: 1, of which 1 were waited for; matrix products, arithmetic and copies ran while one was open for 1% of the time, Pallas kernels for 0%

profile of v1, /device:TPU:0, one launch (start us, length us, event | category | flops | bytes accessed | tf_op | source)
XLA Modules:
  0.0 300.7 jit_solution(1767970717726720955)
XLA Ops:
  7.2 0.0 all-gather.2.cloned.1.call-start
  7.2 20.4 %all_to_all.18 = bf16[8,2,128,256]{3,2,1,0:T(8,128)(2,1)S(1)} all-to-all(bf16[8,2,128,256]{3,2,1,0:T(8,128)(2,1)} %param.4), channel_id=1, replica_groups=mesh['chan'=8,'tile_0'=4,'tile_1'=4] {'chan'}, dimensions={0} | all-to-all | bytes 2097152 | tf_op jit(solution)/shard_map/all_to_all | solution.py:247
  27.6 1.1 copy.20
  28.7 0.0 all-gather.2.cloned.1.call-update
  29.4 1.0 fusion.21
  30.4 0.7 pad_maximum_fusion.steering
  31.0 1.4 fusion.13.picks
  32.4 108.3 %all-gather.2.cloned.1.call-done.voltages = bf16[16,2,128,2048]{3,2,1,0:T(8,128)(2,1)} async-done(((bf16[1,2,128,2048]{3,2,1,0:T(8,128)(2,1)}), bf16[16,2,128,2048]{3,2,1,0:T(8,128)(2,1)}) %all-gather.2.cloned.1.call-update) | async-done | bytes 16777232 | tf_op jit(solution)/shard_map/all_gather | solution.py:249
  140.7 133.9 %shard_map.59 = f32[16,128]{1,0:T(8,128)} custom-call(s32[1]{0:T(128)S(6)} %copy.31.flag, s32[1]{0:T(128)} %bitcast.8.place, bf16[16,2,128,2048]{3,2,1,0:T(8,128)(2,1)} %all-gather.2.cloned.1.call-done.voltages, bf16[32,2048]{1,0:T(8,128)(2,1)} %fusion.13.picks, f32[16,2048]{1,0:T(8,128)} %pad_maximum_fusion.steering), custom_call_target="tpu_custom_call" | custom-call | tf_op jit(solution)/shard_map/pallas_call | solution.py:217
  274.6 1.3 copy.30
  275.9 1.3 constant_dynamic-slice_fusion
  277.2 0.7 copy.19
  277.9 0.0 slice-start
  277.9 0.9 fusion.23
  278.8 0.0 slice-start.1
  278.8 0.0 slice-start.2
  278.8 0.0 slice-start.3
  278.8 7.7 %fusion.4 = f32[1,1,128,2048]{3,2,1,0:T(8,128)S(1)} fusion(bf16[16,2,128,128]{2,3,0,1:T(8,128)(2,1)S(1)} %copy.19, bf16[16,2,128,2048]{3,2,1,0:T(8,128)(2,1)} %all-gather.2.cloned.1.call-done.voltages), kind=kOutput, calls=%fused_computation.4 | convolution fusion | flops 2147483648 | bytes 18874368 | tf_op jit(solution)/shard_map/tpsi,tpsj->ij/dot_general | solution.py:252
  286.5 0.0 slice-done
  286.5 0.0 slice-done.1
  286.5 1.2 slice-done.2
  287.7 1.2 slice-done.3
  288.9 3.5 %fusion.7 = f32[1,1,128,2048]{3,2,1,0:T(8,128)S(1)} fusion(bf16[16,2,128,2048]{3,2,1,0:T(8,128)(2,1)S(1)} %bitcast.26, bf16[16,1,128,128]{2,3,0,1:T(8,128)(2,1)} %get-tuple-element.3, bf16[16,1,128,128]{2,3,0,1:T(8,128)(2,1)S(1)} %get-tuple-element.2), kind=kOutput, calls=%fused_computation.5 | convolution fusion | flops 2148007936 | bytes 18874368 | tf_op jit(solution)/shard_map/tpsi,tpsj->ij/dot_general | solution.py:253
  292.4 1.5 maximum_multiply_fusion
  (1 shorter events, 0.0 us)
Async XLA Ops:
  7.2 133.6 %all-gather.2.cloned.1.call-start = ((), (), s32[]{:S(2)}) async-start(), calls=%async_computation.1 | async-start | bytes 17825792 | tf_op jit(solution)/shard_map/all_gather | solution.py:249
  277.9 8.6 %slice-start = ((s8[16777216]{0:T(1024)(128)(4,1)}), s8[4194304]{0:T(1024)(128)(4,1)S(1)}, s32[]{:S(2)}) async-start(s8[16777216]{0:T(1024)(128)(4,1)} %bitcast.25), calls=%async_computation.2 | async-start | bytes 8388608
  278.8 7.7 %slice-start.1 = ((s8[16777216]{0:T(1024)(128)(4,1)}), s8[4194304]{0:T(1024)(128)(4,1)S(1)}, s32[]{:S(2)}) async-start(s8[16777216]{0:T(1024)(128)(4,1)} %bitcast.25), calls=%async_computation.3 | async-start | bytes 8388608
  278.8 8.9 %slice-start.2 = ((s8[16777216]{0:T(1024)(128)(4,1)}), s8[4194304]{0:T(1024)(128)(4,1)S(1)}, s32[]{:S(2)}) async-start(s8[16777216]{0:T(1024)(128)(4,1)} %bitcast.25), calls=%async_computation.4 | async-start | bytes 8388608
  278.8 10.1 %slice-start.3 = ((s8[16777216]{0:T(1024)(128)(4,1)}), s8[4194304]{0:T(1024)(128)(4,1)S(1)}, s32[]{:S(2)}) async-start(s8[16777216]{0:T(1024)(128)(4,1)} %bitcast.25), calls=%async_computation.5 | async-start | bytes 8388608
Sparse Core Ops, SparseCore 0:
  28.8 111.8 all-gather.1

commit v2 on v1

v2 whole, which is shorter than its diff:
```python
import functools
import math

import jax
import jax.numpy as jnp
from jax import lax
from jax.experimental import pallas as pl
from jax.experimental.pallas import tpu as pltpu
from jax.sharding import Mesh
from jax.sharding import PartitionSpec as P

ARRAY_ELEMENTS = 2048
SNAPSHOT_COUNT = 2048
SUBSPACE_SIZE = 32
BEAM_COUNT = 8
SUB_ITERS = 4
CG_ITERS = 12
TILE = ("tile_0", "tile_1")
TILES = 16
ROWS = 128
WIDE = 256
SPLIT = (32, 96)

diagonal_loading = 0.1
f32 = jnp.float32
bf16 = jnp.bfloat16


def pieces(x, count=3):
    terms = [x.astype(bf16)]
    for _ in range(count - 1):
        x = x - terms[-1].astype(f32)
        terms.append(x.astype(bf16))
    return jnp.concatenate(terms, 0)


def fold(x, count):
    rows = x.shape[0] // count
    total = x[:rows]
    for n in range(1, count):
        total = total + x[n * rows : (n + 1) * rows]
    return total


def plain(a, b):
    return lax.dot_general(a, b, (((1,), (0,)), ((), ())), preferred_element_type=f32)


def turned_dot(a, b):
    return lax.dot_general(a, b, (((1,), (1,)), ((), ())), preferred_element_type=f32)


def tile_through(lhs, matrix, cols, count, sign):
    by_real = fold(plain(lhs[...], matrix[0, :, cols]), count)
    by_imag = fold(plain(lhs[...], matrix[1, :, cols]), count)
    half = by_real.shape[0] // 2
    swapped = jnp.concatenate([-by_imag[half:], by_imag[:half]], 0)
    return by_real + swapped if sign > 0 else by_real - swapped


def column_tiles():
    return [pl.ds(n * WIDE, WIDE) for n in range(ARRAY_ELEMENTS // WIDE)]


def beam_sum(x):
    folded = x[:BEAM_COUNT] + x[BEAM_COUNT:]
    return jnp.sum(folded, axis=1, keepdims=True)


def twice(x):
    return jnp.concatenate([x, x], 0)


def every_group(x):
    x = x + pltpu.roll(x, 64, 1)
    return x + pltpu.roll(x, 32, 1)


def stack_pieces(y):
    blank = jnp.zeros((SUBSPACE_SIZE, y.shape[1]), bf16)
    return jnp.concatenate(
        [pieces(y[:SUBSPACE_SIZE]), blank, pieces(y[SUBSPACE_SIZE:]), blank], 0
    )


def unit_rows(stacked, store):
    size = SUBSPACE_SIZE
    raw = turned_dot(stacked[...], stacked[...])
    top, bottom = fold(raw[: 4 * size], 4), fold(raw[4 * size :], 4)
    g_r = every_group(top[:, : 4 * size] + bottom[:, 4 * size :])
    g_i = every_group(bottom[:, : 4 * size] - top[:, 4 * size :])
    row = lax.broadcasted_iota(jnp.int32, (size, 4 * size), 0)
    lane = lax.broadcasted_iota(jnp.int32, (size, 4 * size), 1)
    a_r = jnp.where(lane < size, g_r, jnp.where(lane - size == row, 1.0, 0.0))
    a_i = jnp.where(lane < size, g_i, 0.0)
    blocks = size // 8
    a_r = [a_r[8 * n : 8 * n + 8] for n in range(blocks)]
    a_i = [a_i[8 * n : 8 * n + 8] for n in range(blocks)]
    within = lax.broadcasted_iota(jnp.int32, (8, 1), 0)
    pivots = []
    for k in range(size):
        own, at = k // 8, k % 8
        pivot = a_r[own][at : at + 1, k : k + 1]
        pivots.append(pivot)
        inverse = 1.0 / pivot
        p_r = a_r[own][at : at + 1] * inverse
        p_i = a_i[own][at : at + 1] * inverse
        for n in range((k + 1) // 8, blocks):
            f_r, f_i = a_r[n][:, k : k + 1], a_i[n][:, k : k + 1]
            if n == own:
                f_r = jnp.where(within > at, f_r, 0.0)
                f_i = jnp.where(within > at, f_i, 0.0)
            a_r[n], a_i[n] = (
                a_r[n] - (f_r * p_r - f_i * p_i),
                a_i[n] - (f_r * p_i + f_i * p_r),
            )
    scale = 1.0 / jnp.sqrt(jnp.concatenate(pivots, 0))
    middle = (lane >= size) & (lane < 2 * size)
    j_r = every_group(jnp.where(middle, jnp.concatenate(a_r, 0) * scale, 0.0))
    j_i = every_group(jnp.where(middle, jnp.concatenate(a_i, 0) * scale, 0.0))
    lhs = pieces(
        jnp.concatenate([jnp.concatenate([j_r, -j_i], 1), jnp.concatenate([j_i, j_r], 1)], 0)
    )
    for cols in column_tiles():
        store(cols, fold(plain(lhs, stacked[:, cols]), 3))


def weights_kernel(
    flag, place, early, late, picks, steering, cov_out, out,
    v, vt, basis, basis_t, wide, seen, narrow, cov, state, sems, out_sems,
):
    inverse_count = 1.0 / SNAPSHOT_COUNT
    tiles = column_tiles()
    sources = (early, late)

    def copy(h, n, part):
        rows = pl.ds(TILES * sum(SPLIT[:h]) + n * SPLIT[h], SPLIT[h])
        return pltpu.make_async_copy(sources[h].at[n, part], v.at[part, rows], sems.at[h, n, part])

    for h in range(2):
        for n in range(TILES):
            for part in range(2):
                copy(h, n, part).start()

    squares = jnp.zeros((8, ARRAY_ELEMENTS), f32)
    for h in range(2):
        for group in range(0, TILES, 4):
            for part in range(2):
                for n in range(group, group + 4):
                    copy(h, n, part).wait()
                start = TILES * sum(SPLIT[:h]) + group * SPLIT[h]
                for first in range(start, start + 4 * SPLIT[h], ROWS):
                    block = v[part, first : first + ROWS, :]
                    vt[part, :, first : first + ROWS] = block.T
                    exact = block.astype(f32)
                    squares = squares + jnp.sum(
                        (exact * exact).reshape(ROWS // 8, 8, ARRAY_ELEMENTS), axis=0
                    )
    power = jnp.sum(jnp.sum(squares, axis=0, keepdims=True), axis=1, keepdims=True)
    load = diagonal_loading * (power * inverse_count) / ARRAY_ELEMENTS

    own = pl.ds(pl.multiple_of(place[0] * ROWS, ROWS), ROWS)

    def covariance_tiles(sweep_index):
        for n in range(2):
            cols = pl.ds(pl.multiple_of((2 * sweep_index + n) * WIDE, WIDE), WIDE)
            lhs = jnp.concatenate([vt[0, own, :], vt[1, own, :]], 0)
            by_real, by_imag = plain(lhs, v[0, :, cols]), plain(lhs, v[1, :, cols])
            cov[0, :, cols] = (by_real[:ROWS] + by_imag[ROWS:]) * inverse_count
            cov[1, :, cols] = (by_real[ROWS:] - by_imag[:ROWS]) * inverse_count

    def cov_copy(part):
        return pltpu.make_async_copy(cov.at[part], cov_out.at[part], out_sems.at[part])

    exact_rows = wide.at[: 2 * SUBSPACE_SIZE]
    for cols in tiles:
        taken_r = plain(picks[...], vt[0, :, cols])
        taken_i = plain(picks[...], vt[1, :, cols])
        exact_rows[:, cols] = jnp.concatenate([taken_r, -taken_i], 0).astype(bf16)
    for cols in tiles:
        basis[:, cols] = stack_pieces(tile_through(exact_rows, v, cols, 1, 1) * inverse_count)

    def to_wide(cols, q):
        wide[:, cols] = pieces(q, 2)

    def sweep(n, carry):
        covariance_tiles(n)
        unit_rows(basis, to_wide)
        for cols in tiles:
            seen[:, cols] = pieces(tile_through(wide, vt, cols, 2, -1), 2)
        for cols in tiles:
            basis[:, cols] = stack_pieces(tile_through(seen, v, cols, 2, 1) * inverse_count)
        return carry

    lax.fori_loop(0, SUB_ITERS - 1, sweep, 0)
    covariance_tiles(SUB_ITERS - 1)
    for part in range(2):
        cov_copy(part).start()
    flagged = flag[0].astype(f32)

    def keep(cols, q):
        basis[:, cols] = stack_pieces(q * flagged)
        basis_t[cols, :] = basis[:, cols].T

    unit_rows(basis, keep)

    def coefficients(cols, x):
        return fold(plain(pieces(x), basis_t[cols, :]), 3)

    def remove(raw):
        half = BEAM_COUNT
        c_r = raw[:half, :128] + raw[half:, 128:]
        c_i = raw[half:, :128] - raw[:half, 128:]
        c = every_group(jnp.concatenate([c_r, c_i], 0))
        crossed = jnp.concatenate([-c[half:], c[:half]], 0)
        both = pieces(jnp.concatenate([c, crossed], 1))
        return jnp.concatenate([fold(plain(both, basis[:, cols]), 3) for cols in tiles], 1)

    source = steering[...]
    state[0] = jnp.zeros_like(source)
    held = remove(sum(coefficients(cols, steering[:, cols]) for cols in tiles))
    clean = source - held
    state[1] = clean
    state[2] = clean
    state[3] = held
    inside = beam_sum(held * held)

    def correlate(write):
        narrow[...] = pieces(state[2])
        total = jnp.zeros((2 * BEAM_COUNT, WIDE), f32)
        for cols in tiles:
            part = tile_through(narrow, vt, cols, 3, -1)
            if write:
                seen[: 6 * BEAM_COUNT, cols] = pieces(part)
            total = total + part * part
        return beam_sum(total)

    def curvature_of(energy, direction, tau):
        return energy * inverse_count + load * (
            beam_sum(direction * direction) + tau * tau * inside
        )

    def iterate(n, carry):
        norm, xi, rho, tau = carry
        energy = correlate(True)
        direction = state[2]
        step = norm / curvature_of(energy, direction, tau)
        state[0] = state[0] + twice(step) * direction
        state[1] = state[1] - twice(step * load) * direction
        xi = xi + step * tau
        rho = rho - step * (load * tau)
        raw = jnp.zeros((2 * BEAM_COUNT, WIDE), f32)
        for cols in tiles:
            mapped = tile_through(seen.at[: 6 * BEAM_COUNT], v, cols, 3, 1) * inverse_count
            raw = raw + coefficients(cols, mapped)
            state[4, :, cols] = mapped
        residual = state[1] - twice(step) * (state[4] - remove(raw))
        state[1] = residual
        fresh = beam_sum(residual * residual) + rho * rho * inside
        ratio = fresh / norm
        state[2] = residual + twice(ratio) * direction
        tau = rho + ratio * tau
        return fresh, xi, rho, tau

    one = jnp.ones((BEAM_COUNT, 1), f32)
    first = (beam_sum(source * source), jnp.zeros((BEAM_COUNT, 1), f32), one, one)
    norm, xi, rho, tau = lax.fori_loop(0, CG_ITERS - 1, iterate, first)
    direction = state[2]
    step = norm / curvature_of(correlate(False), direction, tau)
    solved = state[0] + twice(step) * direction + twice(xi + step * tau) * state[3]
    response = beam_sum(source * solved)
    state[0] = ARRAY_ELEMENTS * solved / twice(response)
    out[...] = state[0, :, own]
    for part in range(2):
        cov_copy(part).wait()


def local_weights(flag, place, early, late, picks, steering, interpret=False):
    vmem = pl.BlockSpec(memory_space=pltpu.VMEM)
    smem = pl.BlockSpec(memory_space=pltpu.SMEM)
    hbm = pl.BlockSpec(memory_space=pl.ANY)
    return pl.pallas_call(
        weights_kernel,
        out_shape=(
            jax.ShapeDtypeStruct((2, ROWS, ARRAY_ELEMENTS), f32),
            jax.ShapeDtypeStruct((2 * BEAM_COUNT, ROWS), f32),
        ),
        in_specs=[smem, smem, hbm, hbm, vmem, vmem],
        out_specs=(hbm, vmem),
        scratch_shapes=[
            pltpu.VMEM((2, SNAPSHOT_COUNT, ARRAY_ELEMENTS), bf16),
            pltpu.VMEM((2, ARRAY_ELEMENTS, SNAPSHOT_COUNT), bf16),
            pltpu.VMEM((8 * SUBSPACE_SIZE, ARRAY_ELEMENTS), bf16),
            pltpu.VMEM((ARRAY_ELEMENTS, 8 * SUBSPACE_SIZE), bf16),
            pltpu.VMEM((4 * SUBSPACE_SIZE, ARRAY_ELEMENTS), bf16),
            pltpu.VMEM((4 * SUBSPACE_SIZE, SNAPSHOT_COUNT), bf16),
            pltpu.VMEM((6 * BEAM_COUNT, ARRAY_ELEMENTS), bf16),
            pltpu.VMEM((2, ROWS, ARRAY_ELEMENTS), f32),
            pltpu.VMEM((5, 2 * BEAM_COUNT, ARRAY_ELEMENTS), f32),
            pltpu.SemaphoreType.DMA((2, TILES, 2)),
            pltpu.SemaphoreType.DMA((2,)),
        ],
        compiler_params=pltpu.CompilerParams(vmem_limit_bytes=58 << 20),
        interpret=interpret,
    )(flag, place, early, late, picks, steering)


def steering_table(beam_entries):
    element_index = jnp.arange(ARRAY_ELEMENTS, dtype=jnp.int32)
    steer_phases = (beam_entries[..., None] * element_index % ARRAY_ELEMENTS).astype(f32) * (
        2.0 * math.pi / ARRAY_ELEMENTS
    )
    return jnp.concatenate([jnp.cos(steer_phases), jnp.sin(steer_phases)], axis=0)


def shards(voltages, rfi_flags, beam_steer_index, start_columns):
    place = lax.axis_index(TILE)
    gathered = []
    for first, rows in zip((0, SPLIT[0]), SPLIT):
        turned = lax.all_to_all(
            voltages[:, :, first : first + rows], "chan", split_axis=0, concat_axis=3, tiled=True
        )
        gathered.append(lax.all_gather(turned[0], TILE, axis=0, tiled=False))
    picks = (start_columns[0][:, None] == jnp.arange(ARRAY_ELEMENTS, dtype=jnp.int32)).astype(bf16)
    steering = steering_table(beam_steer_index[0])
    covariance, weights = local_weights(
        rfi_flags, place[None].astype(jnp.int32), *gathered, picks, steering
    )
    weights = jnp.swapaxes(weights.reshape(1, 2, BEAM_COUNT, ROWS), 1, 2)
    return (covariance[None], weights)


def solution(mesh):
    split = Mesh(mesh.devices.reshape(mesh.shape["chan"], 4, 4), ("chan", "tile_0", "tile_1"))
    return jax.shard_map(
        shards,
        mesh=split,
        in_specs=(P(None, None, TILE, "chan"), P("chan"), P("chan", None), P("chan", None)),
        out_specs=(P("chan", None, TILE, None), P("chan", None, None, TILE)),
        check_vma=False,
    )
```

time: 302 us -> 303 us (level)
  waiting for transfers between devices: 108 us -> 124 us
  matrix products: 11.1 us -> 0 us
  blocking collectives: 20.4 us -> 27.3 us
  Pallas kernels: 134 us -> 129 us
  other arithmetic: 5.45 us -> 1.74 us
    all_gather x1 -> x2, waiting for transfers between devices: 108 us -> 124 us  [shards(): gathered.append(lax.all_gather(turned[0], TILE, axis=0, tiled=False))]
    dot_general x2 -> x0, matrix products: 11.1 us -> none  [the longest x1 7.68 us: shards(): jnp.einsum('tpsi,tpsj->ij', own, gathered, preferred_element_type=f32)]
    all_to_all x1 -> x2, blocking collectives: 20.4 us -> 27.3 us  [shards(): lax.all_to_all(voltages[:, :, first:first + rows], 'chan', split_axis=0,...]
    pallas_call x1, Pallas kernels: 134 us -> 129 us  [local_weights(): pl.pallas_call(weights_kernel, out_shape=(jax.ShapeDtypeStruct((2, ROWS,...]
    unnamed x9 -> x4, local copies, waits for them, and re-layouts: 3.05 us -> 0.01 us
  transfers between devices with their start and end apart: 1 -> 2, of which waited for: 1 -> 2; matrix products, arithmetic and copies ran while one was open for 1% -> 1% of each run, Pallas kernels for 0% -> 0%
where the time goes in v2:
time: 303 us
  Pallas kernels  129 us (43%)
  waiting for transfers between devices  124 us (41%)
  blocking collectives  27.3 us (9%)
  between operations  14.7 us (5%)
  local copies, waits for them, and re-layouts  5.16 us (2%)
    pallas_call x1, Pallas kernels, local_weights(): pl.pallas_call(weights_kernel, out_shape=(jax.ShapeDtypeStruct((2, ROWS,...  129 us
    all_gather x2, waiting for transfers between devices, shards(): gathered.append(lax.all_gather(turned[0], TILE, axis=0, tiled=False))  124 us
    all_to_all x2, blocking collectives, shards(): lax.all_to_all(voltages[:, :, first:first + rows], 'chan', split_axis=0,...  27.3 us
  transfers between devices with their start and end apart: 2, of which 2 were waited for; matrix products, arithmetic and copies ran while one was open for 1% of the time, Pallas kernels for 0%

profile of v2, /device:TPU:0, one launch (start us, length us, event | category | flops | bytes accessed | tf_op | source)
XLA Modules:
  0.0 302.5 jit_solution(17009947172297900821)
XLA Ops:
  7.2 0.0 copy-start
  7.2 0.0 copy-start.1
  7.2 0.0 all-gather.3.cloned.1.call-start
  7.2 1.0 slice.6
  8.2 11.7 %all_to_all.36 = bf16[8,2,32,256]{3,2,1,0:T(8,128)(2,1)S(1)} all-to-all(bf16[8,2,32,256]{3,2,1,0:T(8,128)(2,1)S(1)} %slice.6), channel_id=1, replica_groups=mesh['chan'=8,'tile_0'=4,'tile_1'=4] {'chan'}, dimensions={0} | all-to-all | bytes 524288 | tf_op jit(solution)/shard_map/all_to_all | solution.py:320
  19.9 0.7 copy.12
  20.6 0.0 all-gather.3.cloned.1.call-update
  20.7 0.0 all-gather.5.cloned.1.call-start
  20.7 1.2 slice.7
  21.9 15.6 %all_to_all.37 = bf16[8,2,96,256]{3,2,1,0:T(8,128)(2,1)S(1)} all-to-all(bf16[8,2,96,256]{3,2,1,0:T(8,128)(2,1)S(1)} %slice.7), channel_id=1, replica_groups=mesh['chan'=8,'tile_0'=4,'tile_1'=4] {'chan'}, dimensions={0} | all-to-all | bytes 1572864 | tf_op jit(solution)/shard_map/all_to_all | solution.py:320
  37.5 1.0 copy.13
  38.5 0.0 all-gather.5.cloned.1.call-update
  39.1 0.0 copy-done
  39.2 0.3 fusion.8
  39.5 0.7 pad_maximum_fusion.steering
  40.2 0.0 copy-done.1
  40.2 0.7 fusion.picks
  40.9 32.0 %all-gather.3.cloned.1.call-done.early = bf16[16,2,32,2048]{3,2,1,0:T(8,128)(2,1)} async-done(((bf16[1,2,32,2048]{3,2,1,0:T(8,128)(2,1)}), bf16[16,2,32,2048]{3,2,1,0:T(8,128)(2,1)}) %all-gather.3.cloned.1.call-update) | async-done | bytes 4194320 | tf_op jit(solution)/shard_map/all_gather | solution.py:323
  72.9 92.2 %all-gather.5.cloned.1.call-done.late = bf16[16,2,96,2048]{3,2,1,0:T(8,128)(2,1)} async-done(((bf16[1,2,96,2048]{3,2,1,0:T(8,128)(2,1)}), bf16[16,2,96,2048]{3,2,1,0:T(8,128)(2,1)}) %all-gather.5.cloned.1.call-update) | async-done | bytes 12582928 | tf_op jit(solution)/shard_map/all_gather | solution.py:323
  165.1 129.3 %shard_map.59 = (f32[2,128,2048]{2,1,0:T(8,128)}, f32[16,128]{1,0:T(8,128)}) custom-call(s32[1]{0:T(128)S(6)} %copy.16.flag, s32[1]{0:T(128)} %bitcast.place, bf16[16,2,32,2048]{3,2,1,0:T(8,128)(2,1)} %all-gather.3.cloned.1.call-done.early, bf16[16,2,96,2048]{3,2,1,0:T(8,128)(2,1)} %all-gather.5.cloned.1.call-done.late, bf16[32,2048]{1,0:T(8,128)(2,1)} %fusion.picks, ...), custom_call_target="tpu_custom_call" | custom-call | tf_op jit(solution)/shard_map/pallas_call | solution.py:282
  294.4 1.3 copy.15
Async XLA Ops:
  7.2 32.0 %copy-start = (s32[1,8]{1,0:T(1,128)S(1)}, s32[1,8]{1,0:T(1,128)}, u32[]{:S(2)}) copy-start(s32[1,8]{1,0:T(1,128)} %param.6) | copy-start | bytes 100
  7.2 33.0 %copy-start.1 = (s32[1,32]{1,0:T(1,128)S(1)}, s32[1,32]{1,0:T(1,128)}, u32[]{:S(2)}) copy-start(s32[1,32]{1,0:T(1,128)} %param.7) | copy-start | bytes 388
  7.2 65.7 %all-gather.3.cloned.1.call-start = ((), (), s32[]{:S(2)}) async-start(), calls=%async_computation.2 | async-start | bytes 4456448 | tf_op jit(solution)/shard_map/all_gather | solution.py:323
  20.7 144.4 %all-gather.5.cloned.1.call-start = ((), (), s32[]{:S(2)}) async-start(), calls=%async_computation.3 | async-start | bytes 13369344 | tf_op jit(solution)/shard_map/all_gather | solution.py:323
Sparse Core Ops, SparseCore 0:
  20.8 52.0 all-gather.2
  75.6 89.4 all-gather.4

commit v3 on v2

--- a/solution.py
+++ b/solution.py
@@ -19,7 +19,6 @@
 TILES = 16
 ROWS = 128
 WIDE = 256
-SPLIT = (32, 96)
 
 diagonal_loading = 0.1
 f32 = jnp.float32
@@ -126,36 +125,28 @@
 
 
 def weights_kernel(
-    flag, place, early, late, picks, steering, cov_out, out,
+    flag, place, gathered, picks, steering, cov_out, out,
     v, vt, basis, basis_t, wide, seen, narrow, cov, state, sems, out_sems,
 ):
     inverse_count = 1.0 / SNAPSHOT_COUNT
     tiles = column_tiles()
-    sources = (early, late)
-
-    def copy(h, n, part):
-        rows = pl.ds(TILES * sum(SPLIT[:h]) + n * SPLIT[h], SPLIT[h])
-        return pltpu.make_async_copy(sources[h].at[n, part], v.at[part, rows], sems.at[h, n, part])
-
-    for h in range(2):
-        for n in range(TILES):
-            for part in range(2):
-                copy(h, n, part).start()
+
+    def copy(n, part):
+        rows = pl.ds(n * ROWS, ROWS)
+        return pltpu.make_async_copy(gathered.at[n, part], v.at[part, rows], sems.at[n, part])
+
+    for n in range(TILES):
+        for part in range(2):
+            copy(n, part).start()
 
     squares = jnp.zeros((8, ARRAY_ELEMENTS), f32)
-    for h in range(2):
-        for group in range(0, TILES, 4):
-            for part in range(2):
-                for n in range(group, group + 4):
-                    copy(h, n, part).wait()
-                start = TILES * sum(SPLIT[:h]) + group * SPLIT[h]
-                for first in range(start, start + 4 * SPLIT[h], ROWS):
-                    block = v[part, first : first + ROWS, :]
-                    vt[part, :, first : first + ROWS] = block.T
-                    exact = block.astype(f32)
-                    squares = squares + jnp.sum(
-                        (exact * exact).reshape(ROWS // 8, 8, ARRAY_ELEMENTS), axis=0
-                    )
+    for n in range(TILES):
+        for part in range(2):
+            copy(n, part).wait()
+            block = v[part, n * ROWS : (n + 1) * ROWS, :]
+            vt[part, :, n * ROWS : (n + 1) * ROWS] = block.T
+            exact = block.astype(f32)
+            squares = squares + jnp.sum((exact * exact).reshape(ROWS // 8, 8, ARRAY_ELEMENTS), axis=0)
     power = jnp.sum(jnp.sum(squares, axis=0, keepdims=True), axis=1, keepdims=True)
     load = diagonal_loading * (power * inverse_count) / ARRAY_ELEMENTS
 
@@ -275,7 +266,7 @@
         cov_copy(part).wait()
 
 
-def local_weights(flag, place, early, late, picks, steering, interpret=False):
+def local_weights(flag, place, gathered, picks, steering, interpret=False):
     vmem = pl.BlockSpec(memory_space=pltpu.VMEM)
     smem = pl.BlockSpec(memory_space=pltpu.SMEM)
     hbm = pl.BlockSpec(memory_space=pl.ANY)
@@ -285,7 +276,7 @@
             jax.ShapeDtypeStruct((2, ROWS, ARRAY_ELEMENTS), f32),
             jax.ShapeDtypeStruct((2 * BEAM_COUNT, ROWS), f32),
         ),
-        in_specs=[smem, smem, hbm, hbm, vmem, vmem],
+        in_specs=[smem, smem, hbm, vmem, vmem],
         out_specs=(hbm, vmem),
         scratch_shapes=[
             pltpu.VMEM((2, SNAPSHOT_COUNT, ARRAY_ELEMENTS), bf16),
@@ -297,12 +288,12 @@
             pltpu.VMEM((6 * BEAM_COUNT, ARRAY_ELEMENTS), bf16),
             pltpu.VMEM((2, ROWS, ARRAY_ELEMENTS), f32),
             pltpu.VMEM((5, 2 * BEAM_COUNT, ARRAY_ELEMENTS), f32),
-            pltpu.SemaphoreType.DMA((2, TILES, 2)),
+            pltpu.SemaphoreType.DMA((TILES, 2)),
             pltpu.SemaphoreType.DMA((2,)),
         ],
         compiler_params=pltpu.CompilerParams(vmem_limit_bytes=58 << 20),
         interpret=interpret,
-    )(flag, place, early, late, picks, steering)
+    )(flag, place, gathered, picks, steering)
 
 
 def steering_table(beam_entries):
@@ -315,16 +306,12 @@
 
 def shards(voltages, rfi_flags, beam_steer_index, start_columns):
     place = lax.axis_index(TILE)
-    gathered = []
-    for first, rows in zip((0, SPLIT[0]), SPLIT):
-        turned = lax.all_to_all(
-            voltages[:, :, first : first + rows], "chan", split_axis=0, concat_axis=3, tiled=True
-        )
-        gathered.append(lax.all_gather(turned[0], TILE, axis=0, tiled=False))
+    turned = lax.all_to_all(voltages, "chan", split_axis=0, concat_axis=3, tiled=True)
+    gathered = lax.all_gather(turned[0], TILE, axis=0, tiled=False)
     picks = (start_columns[0][:, None] == jnp.arange(ARRAY_ELEMENTS, dtype=jnp.int32)).astype(bf16)
     steering = steering_table(beam_steer_index[0])
     covariance, weights = local_weights(
-        rfi_flags, place[None].astype(jnp.int32), *gathered, picks, steering
+        rfi_flags, place[None].astype(jnp.int32), gathered, picks, steering
     )
     weights = jnp.swapaxes(weights.reshape(1, 2, BEAM_COUNT, ROWS), 1, 2)
     return (covariance[None], weights)

time: 303 us -> 279 us (0.921)
  waiting for transfers between devices: 124 us -> 108 us
  blocking collectives: 27.3 us -> 20.4 us
    all_gather x2 -> x1, waiting for transfers between devices: 124 us -> 108 us  [shards(): gathered = lax.all_gather(turned[0], TILE, axis=0, tiled=False)]
    all_to_all x2 -> x1, blocking collectives: 27.3 us -> 20.4 us  [shards(): lax.all_to_all(voltages, 'chan', split_axis=0, concat_axis=3, tiled=True)]
  transfers between devices with their start and end apart: 2 -> 1, of which waited for: 2 -> 1; matrix products, arithmetic and copies ran while one was open for 1% -> 1% of each run, Pallas kernels for 0% -> 0%
where the time goes in v3:
time: 279 us
  Pallas kernels  130 us (47%)
  waiting for transfers between devices  108 us (39%)
  blocking collectives  20.4 us (7%)
  between operations  14.7 us (5%)
  other arithmetic  3.07 us (1%)
    pallas_call x1, Pallas kernels, local_weights(): pl.pallas_call(weights_kernel, out_shape=(jax.ShapeDtypeStruct((2, ROWS,...  130 us
    all_gather x1, waiting for transfers between devices, shards(): gathered = lax.all_gather(turned[0], TILE, axis=0, tiled=False)  108 us
    all_to_all x1, blocking collectives, shards(): lax.all_to_all(voltages, 'chan', split_axis=0, concat_axis=3, tiled=True)  20.4 us
  transfers between devices with their start and end apart: 1, of which 1 were waited for; matrix products, arithmetic and copies ran while one was open for 1% of the time, Pallas kernels for 0%

profile of v3, /device:TPU:0, one launch (start us, length us, event | category | flops | bytes accessed | tf_op | source)
XLA Modules:
  0.0 278.6 jit_solution(4970359376194570493)
XLA Ops:
  7.2 0.0 all-gather.2.cloned.1.call-start
  7.2 20.4 %all_to_all.18 = bf16[8,2,128,256]{3,2,1,0:T(8,128)(2,1)S(1)} all-to-all(bf16[8,2,128,256]{3,2,1,0:T(8,128)(2,1)} %param.4), channel_id=1, replica_groups=mesh['chan'=8,'tile_0'=4,'tile_1'=4] {'chan'}, dimensions={0} | all-to-all | bytes 2097152 | tf_op jit(solution)/shard_map/all_to_all | solution.py:309
  27.6 1.1 copy.10
  28.7 0.0 all-gather.2.cloned.1.call-update
  29.4 1.0 fusion.8
  30.4 0.7 pad_maximum_fusion.steering
  31.1 1.4 fusion.picks
  32.5 108.3 %all-gather.2.cloned.1.call-done.gathered = bf16[16,2,128,2048]{3,2,1,0:T(8,128)(2,1)} async-done(((bf16[1,2,128,2048]{3,2,1,0:T(8,128)(2,1)}), bf16[16,2,128,2048]{3,2,1,0:T(8,128)(2,1)}) %all-gather.2.cloned.1.call-update) | async-done | bytes 16777232 | tf_op jit(solution)/shard_map/all_gather | solution.py:310
  140.7 129.7 %shard_map.59 = (f32[2,128,2048]{2,1,0:T(8,128)}, f32[16,128]{1,0:T(8,128)}) custom-call(s32[1]{0:T(128)S(6)} %copy.13.flag, s32[1]{0:T(128)} %bitcast.place, bf16[16,2,128,2048]{3,2,1,0:T(8,128)(2,1)} %all-gather.2.cloned.1.call-done.gathered, bf16[32,2048]{1,0:T(8,128)(2,1)} %fusion.picks, f32[16,2048]{1,0:T(8,128)} %pad_maximum_fusion.steering), custom_call_target="tpu_custom_call" | custom-call | tf_op jit(solution)/shard_map/pallas_call | solution.py:273
  270.5 1.3 copy.12
Async XLA Ops:
  7.2 133.6 %all-gather.2.cloned.1.call-start = ((), (), s32[]{:S(2)}) async-start(), calls=%async_computation.1 | async-start | bytes 17825792 | tf_op jit(solution)/shard_map/all_gather | solution.py:310
Sparse Core Ops, SparseCore 0:
  28.8 111.8 all-gather.1
